TPU v7x, 32 devices: a whole 2x2x4 slice. The times are simulated.
32 devices in a mesh: job: 2 (over y), aux: 16 (over z, x, core).
Axes of the slice: x: 2, y: 2, z: 4, core: 2. Of those that a mesh axis runs over, the one named last changes fastest.
Arguments:
- ints_ov: bfloat16 [256, 384, 384], P(('job', 'aux')), parts along dimension 0, may hold values from -0.3125 to 0.3125
- ints_oo: bfloat16 [256, 2, 384], P(('job', 'aux')), parts along dimension 0, may hold values from -1.5 to 1.5
- trial: bfloat16 [64, 4, 384], P('job'), parts along dimension 0, may hold values from -6 to 6
- occ_energy: float32 [64], P('job'), parts along dimension 0, may hold values from -1 to -0.2
- vir_energy: float32 [32000], P('job'), parts along dimension 0, may hold values from 0.2 to 2.5
- root_shift: float32 [8], P('job'), parts along dimension 0, may hold values from 0.1 to 0.6
- vir_blocks: int32 [32, 3], P('job'), parts along dimension 0, may hold values from 0 to 124, as said below
- pair_list: int32 [32, 4, 2], P('job'), parts along dimension 0, may hold values from 0 to 31, as said below
- pair_count: int32 [32], P('job'), parts along dimension 0, may hold values from 2 to 4, as said below
Outputs:
- sigma: float32 [64, 4, 384], P(('job', 'aux')), parts along dimension 0
There are 2 independent parts, one for each index of `job`. A program takes and returns all parts, laid end to end along the dimension named above; each array names one. Nothing has to cross between parts.
Inputs may be any that keep to these rules, and one draw needn't show every extreme that they name: `pair_count`: some domain has 4 live pairs. `pair_list`: for domain d all 4 slots hold distinct pairs (i, j): i an occupied of domain d (d * 2 to d * 2 + 1) and j an occupied of one of the domains d + 1 to d + 3, taken cyclically modulo 16; slots from pair_count[d] on are not live. `vir_blocks`: the blocks of one domain are distinct.
All inputs are finite; a program needn't handle non-finite values.
Results may differ from a plain program's by a relative error of at most 0.00036.
Values may be sent and summed in bfloat16 or wider, within the bound.
A program may use at most 128 MiB of HBM per device.

v0:
```python
import functools

import jax
import jax.numpy as jnp
from jax import lax
from jax.experimental import pallas as pl
from jax.experimental.pallas import tpu as pltpu
from jax.sharding import PartitionSpec as P

F32 = jnp.float32
BF16 = jnp.bfloat16
LANES = 128


def split_high_low(value):
    high = value.astype(BF16).astype(F32)
    return high, (value - high).astype(BF16).astype(F32)


def sigma_kernel(
    ndomain, span, slot_count, occ_domain, root_count,
    ints_hbm, couple_hbm, trial_hbm, level_hbm, occ_energy, root_shift, pair_count, vir_blocks, pairs,
    out_ref,
    ints, couple, trial, level_table, levels_col, mixed_own, mixed_far, doubles, stage, landed,
    ints_sem, small_sem, send_sem, recv_sem,
):
    me = lax.axis_index("aux")
    slab_rows, fitting, virt = ints.shape
    width_blocks = virt // LANES
    rows = occ_domain * root_count

    def ahead(steps):
        return lax.rem(me + steps, ndomain)

    barrier = pltpu.get_barrier_semaphore()
    for steps in range(1, span):
        for other in (ahead(steps), ahead(ndomain - steps)):
            pl.semaphore_signal(
                barrier, inc=1, device_id={"aux": other}, device_id_type=pl.DeviceIdType.MESH
            )

    small = [
        pltpu.make_async_copy(couple_hbm, couple, small_sem.at[0]),
        pltpu.make_async_copy(level_hbm, level_table, small_sem.at[1]),
    ]
    for steps in range(span):
        small.append(
            pltpu.make_async_copy(
                trial_hbm.at[pl.ds(ahead(steps) * occ_domain, occ_domain)],
                trial.at[pl.ds(steps * occ_domain, occ_domain)],
                small_sem.at[2 + steps],
            )
        )
    for copy in small:
        copy.start()
    big = [pltpu.make_async_copy(ints_hbm.at[row], ints.at[row], ints_sem.at[row]) for row in range(slab_rows)]
    for copy in big:
        copy.start()
    for copy in small:
        copy.wait()

    def level_rows(relative):
        return [level_table[pl.ds(vir_blocks[block, ahead(relative)], 1), :] for block in range(width_blocks)]

    for block, row in enumerate(level_rows(0)):
        levels_col[pl.ds(block * LANES, LANES), :] = jnp.broadcast_to(row, (LANES, LANES)).T

    row_index = lax.broadcasted_iota(jnp.int32, (rows, 1), 0)

    def trial_rows(relative):
        return jnp.concatenate(
            [trial[relative * occ_domain + own].astype(F32) for own in range(occ_domain)], axis=0
        )

    def couple_rows(slab_row):
        values = couple[slab_row].astype(F32)
        result = jnp.broadcast_to(values[0:1], (rows, fitting))
        for own in range(1, occ_domain):
            result = jnp.where(row_index >= own * root_count, values[own : own + 1], result)
        return result.astype(BF16)

    couple_all = [couple_rows(row) for row in range(slab_rows)]
    own_couple = jnp.concatenate(couple_all[:occ_domain], axis=0)
    far_couple = jnp.concatenate(couple_all[occ_domain:], axis=0)
    far_rows = slab_rows - occ_domain
    for row in range(slab_rows):
        big[row].wait()
        if row < occ_domain:
            mixed = jnp.dot(far_couple, ints[row], preferred_element_type=F32)
            for far in range(far_rows):
                mixed_own[row * far_rows + far] = mixed[far * rows : (far + 1) * rows]
        else:
            mixed = jnp.dot(own_couple, ints[row], preferred_element_type=F32)
            for own in range(occ_domain):
                mixed_far[own * far_rows + row - occ_domain] = mixed[own * rows : (own + 1) * rows]

    trial_first = trial_rows(0)
    live_slots = pair_count[me]
    right_root = lax.broadcasted_iota(jnp.int32, (4 * rows, 1), 0) % root_count
    totals = [jnp.zeros((rows, virt), F32) for _ in range(span)]
    weights = []
    for slot in range(slot_count):
        occ_first = pairs[slot, 0, me]
        occ_second = pairs[slot, 1, me]
        relative = lax.rem(occ_second // occ_domain - me + ndomain, ndomain)
        relative = jnp.maximum(jnp.minimum(relative, span - 1), 1)
        own = lax.rem(occ_first, occ_domain)
        place = own * far_rows + (relative - 1) * occ_domain + lax.rem(occ_second, occ_domain)
        live = live_slots > slot

        first_high, first_low = split_high_low(mixed_own[place])
        second_high, second_low = split_high_low(mixed_far[place])
        trial_second = trial_rows(relative)
        left = jnp.concatenate([trial_first, trial_first, first_high, first_low], axis=0).T.astype(BF16)
        right = jnp.concatenate([second_high, second_low, trial_second, trial_second], axis=0)
        right = jnp.concatenate(
            [jnp.where(right_root == root, right, 0.0) for root in range(root_count)], axis=1
        ).astype(BF16)
        first_pair = jnp.concatenate([first_high, first_low], axis=0).astype(BF16)
        level_row = jnp.concatenate(level_rows(relative), axis=1) - occ_energy[occ_first] - occ_energy[occ_second]
        level_row = jnp.concatenate([level_row - root_shift[root] for root in range(root_count)], axis=1)
        level_col = jnp.concatenate([levels_col[...]] * (width_blocks * root_count), axis=1)

        coupled = jnp.dot(left, right, preferred_element_type=F32)
        answer = (coupled / (level_col + level_row)).astype(BF16)
        doubles[slot] = answer
        weights.append(right[: 2 * rows])
        part = jnp.dot(first_pair, answer, preferred_element_type=F32)
        part = part[:rows] + part[rows:]
        second = jnp.zeros((rows, virt), F32)
        for root in range(root_count):
            second += jnp.where(
                row_index % root_count == root, part[:, root * virt : (root + 1) * virt], 0.0
            )
        for steps in range(1, span):
            totals[steps] += jnp.where(jnp.logical_and(live, relative == steps), second, 0.0)

    for steps in range(1, span):
        stage[steps - 1] = totals[steps]
    pl.semaphore_wait(barrier, 2 * (span - 1))
    copies = []
    for steps in range(1, span):
        copy = pltpu.make_async_remote_copy(
            src_ref=stage.at[steps - 1],
            dst_ref=landed.at[steps - 1],
            send_sem=send_sem.at[steps - 1],
            recv_sem=recv_sem.at[steps - 1],
            device_id={"aux": ahead(steps)},
            device_id_type=pl.DeviceIdType.MESH,
        )
        copy.start()
        copies.append(copy)
    result = totals[0]
    for slot in range(slot_count):
        first = lax.dot_general(
            weights[slot], doubles[slot], (((1,), (1,)), ((), ())), preferred_element_type=F32
        )
        result += jnp.where(live_slots > slot, first[:rows] + first[rows:], 0.0)
    for copy in copies:
        copy.wait()
    for steps in range(1, span):
        result = result + landed[steps - 1]
    for own in range(occ_domain):
        out_ref[own] = result[own * root_count : (own + 1) * root_count]


def per_device(
    ints_ov, ints_oo, trial, occ_energy, vir_energy, root_shift, vir_blocks, pair_list, pair_count
):
    slab_rows, fitting, virt = ints_ov.shape
    occ_domain = ints_oo.shape[1]
    root_count = trial.shape[1]
    slot_count = pair_list.shape[1]
    span = slab_rows // occ_domain
    rows = occ_domain * root_count
    level_table = vir_energy.reshape(-1, LANES)
    anywhere = pl.BlockSpec(memory_space=pl.ANY)
    scalars = pl.BlockSpec(memory_space=pltpu.SMEM)
    return pl.pallas_call(
        functools.partial(
            sigma_kernel, lax.axis_size("aux"), span, slot_count, occ_domain, root_count
        ),
        out_shape=jax.ShapeDtypeStruct((occ_domain, root_count, virt), F32),
        in_specs=[anywhere] * 4 + [scalars] * 5,
        out_specs=pl.BlockSpec(memory_space=pltpu.VMEM),
        scratch_shapes=[
            pltpu.VMEM(ints_ov.shape, BF16),
            pltpu.VMEM(ints_oo.shape, BF16),
            pltpu.VMEM((span * occ_domain, root_count, virt), BF16),
            pltpu.VMEM(level_table.shape, F32),
            pltpu.VMEM((virt, LANES), F32),
            pltpu.VMEM((occ_domain * (slab_rows - occ_domain), rows, virt), F32),
            pltpu.VMEM((occ_domain * (slab_rows - occ_domain), rows, virt), F32),
            pltpu.VMEM((slot_count, virt, root_count * virt), BF16),
            pltpu.VMEM((span - 1, rows, virt), F32),
            pltpu.VMEM((span - 1, rows, virt), F32),
            pltpu.SemaphoreType.DMA((slab_rows,)),
            pltpu.SemaphoreType.DMA((2 + span,)),
            pltpu.SemaphoreType.DMA((span - 1,)),
            pltpu.SemaphoreType.DMA((span - 1,)),
        ],
        compiler_params=pltpu.CompilerParams(collective_id=0, has_side_effects=True),
        name="sigma",
    )(
        ints_ov, ints_oo, trial, level_table, occ_energy, root_shift, pair_count, vir_blocks.T,
        pair_list.transpose(1, 2, 0),
    )


def solution(mesh):
    in_specs = (
        P(("job", "aux"), None, None),
        P(("job", "aux"), None, None),
        P("job", None, None),
        P("job"),
        P("job"),
        P("job"),
        P("job", None),
        P("job", None, None),
        P("job"),
    )
    out_specs = P(("job", "aux"), None, None)
    return jax.shard_map(
        per_device, mesh=mesh, in_specs=in_specs, out_specs=out_specs, check_vma=False
    )
```

profile of v0, /device:TPU:0, one launch (start us, length us, event | category | flops | bytes accessed | tf_op | source)
XLA Modules:
  0.0 16.6 jit_solution(12785303498941207405)
XLA Ops:
  0.0 15.3 %sigma.1 = f32[2,4,384]{2,1,0:T(4,128)} custom-call(bf16[8,384,384]{2,1,0:T(8,128)(2,1)} %ints_hbm.1, bf16[8,2,384]{2,1,0:T(2,128)(2,1)} %couple_hbm.1, bf16[32,4,384]{2,1,0:T(4,128)(2,1)} %trial_hbm.1, f32[125,128]{1,0:T(8,128)} %bitcast.3, f32[32]{0:T(128)} %occ_energy.1, f32[4]{0:T(128)} %root_shift.1, s32[16]{0:T(128)} %pair_count.1, s32[3,16]{1,0:T(4,128)} %bitcast.5, ...), custom_call_target="tpu_custom_call" | custom-call | tf_op jit(solution)/shard_map/sigma/pallas_call | solution.py:179
  15.3 1.3 %copy.11 = f32[2,4,384]{2,1,0:T(4,128)} copy(f32[2,4,384]{2,1,0:T(4,128)} %sigma.1) | data formatting | bytes 24576
where the time goes:
time: 16.9 us; the launch traced here: 16.6 us
  Pallas kernels  15.3 us (91%)
  local copies, waits for them, and re-layouts  1.31 us (8%)
    pallas_call x1, Pallas kernels, per_device(): pl.pallas_call(functools.partial(sigma_kernel, lax.axis_size('aux'), span...  15.3 us
    unnamed x1, local copies, waits for them, and re-layouts  1.31 us

commit v1 on v0

v1 whole, which is shorter than its diff:
```python
import functools

import jax
import jax.numpy as jnp
from jax import lax
from jax.experimental import pallas as pl
from jax.experimental.pallas import tpu as pltpu
from jax.sharding import PartitionSpec as P

F32 = jnp.float32
BF16 = jnp.bfloat16
LANES = 128


def group_sums(parts):
    rows = parts[0].shape[0]
    index = lax.broadcasted_iota(jnp.int32, parts[0].shape, 0)
    step = 1
    while len(parts) > 1:
        low = (index // step) % 2 == 0
        parts = [
            jnp.where(low, even, pltpu.roll(odd, step, 0)) + jnp.where(low, pltpu.roll(even, rows - step, 0), odd)
            for even, odd in zip(parts[::2], parts[1::2])
        ]
        step *= 2
    return parts[0]


def sigma_kernel(
    ndomain, span, slot_count, occ_domain, root_count,
    ints_hbm, couple_hbm, trial_hbm, level_hbm, occ_hbm, shift_hbm, count_hbm, blocks_hbm, pairs_hbm,
    out_ref,
    ints, couple, trial, level_table, occ_energy, root_shift, pair_count, vir_blocks, pairs,
    levels_col, trial_f32, mixed, recip, stage, landed,
    ints_sem, small_sem, send_sem, recv_sem,
):
    me = lax.axis_index("aux")
    slab_rows, fitting, virt = ints.shape
    width_blocks = virt // LANES
    rows = occ_domain * root_count
    terms = 2 * occ_domain

    def ahead(steps):
        return lax.rem(me + steps, ndomain)

    scalars = [
        pltpu.make_async_copy(src, dst, small_sem.at[at])
        for at, (src, dst) in enumerate(
            [
                (level_hbm, level_table), (blocks_hbm, vir_blocks), (pairs_hbm, pairs), (occ_hbm, occ_energy),
                (shift_hbm, root_shift), (count_hbm, pair_count), (couple_hbm, couple),
            ]
        )
    ]
    for copy in scalars:
        copy.start()
    trial_sem = small_sem.at[len(scalars)]
    for steps in range(span):
        pltpu.make_async_copy(
            trial_hbm.at[pl.ds(ahead(steps) * occ_domain, occ_domain)],
            trial.at[pl.ds(steps * occ_domain, occ_domain)],
            trial_sem,
        ).start()
    big = pltpu.make_async_copy(ints_hbm, ints, ints_sem)
    big.start()

    barrier = pltpu.get_barrier_semaphore()
    for steps in range(1, span):
        for other in (ahead(steps), ahead(ndomain - steps)):
            pl.semaphore_signal(
                barrier, inc=1, device_id={"aux": other}, device_id_type=pl.DeviceIdType.MESH
            )

    for copy in scalars:
        copy.wait()
    pltpu.make_async_copy(trial_hbm.at[pl.ds(0, span * occ_domain)], trial, trial_sem).wait()

    def level_rows(relative):
        return [level_table[pl.ds(vir_blocks[block, ahead(relative)], 1), :] for block in range(width_blocks)]

    for block, row in enumerate(level_rows(0)):
        levels_col[pl.ds(block * LANES, LANES), :] = jnp.broadcast_to(row, (LANES, LANES)).T

    slots = []
    for slot in range(slot_count):
        occ_first = pairs[slot, 0, me]
        occ_second = pairs[slot, 1, me]
        relative = lax.rem(occ_second // occ_domain - me + ndomain, ndomain)
        relative = jnp.maximum(jnp.minimum(relative, span - 1), 1)
        first = lax.rem(occ_first, occ_domain)
        second = relative * occ_domain + lax.rem(occ_second, occ_domain)
        slots.append((relative, first, second, occ_energy[occ_first] + occ_energy[occ_second]))

    col = jnp.concatenate([levels_col[...]] * width_blocks, axis=1)
    for slot, (relative, first, second, energy) in enumerate(slots):
        level_row = jnp.concatenate(level_rows(relative), axis=1) - energy
        for root in range(0, root_count, 2):
            dens = [col + (level_row - root_shift[at]) for at in range(root, min(root + 2, root_count))]
            if len(dens) == 2:
                both = 1.0 / (dens[0] * dens[1])
                values = [both * dens[1], both * dens[0]]
            else:
                values = [1.0 / dens[0]]
            for at, value in enumerate(values):
                recip[slot, :, pl.ds((root + at) * virt, virt)] = value.astype(BF16)

    for relative in range(span):
        for own in range(occ_domain):
            trial_f32[relative, pl.ds(own * root_count, root_count), :] = trial[relative * occ_domain + own].astype(F32)
    couple_all = jnp.concatenate([couple[row].astype(F32) for row in range(slab_rows)], axis=0).astype(BF16)

    big.wait()
    for row in range(0, slab_rows, 2):
        pair = jnp.concatenate([ints[row], ints[row + 1]], axis=1)
        both = jnp.dot(couple_all, pair, preferred_element_type=F32)
        mixed[row] = both[:, :virt]
        mixed[row + 1] = both[:, virt:]

    index = lax.broadcasted_iota(jnp.int32, (rows, virt), 0)
    low_bit = index % occ_domain == 0
    own_side = (index // occ_domain) % 2 == 0
    high_bit = index // terms == 0

    def pick(mask, values):
        return jnp.where(mask, jnp.broadcast_to(values[0], (rows, virt)), jnp.broadcast_to(values[1], (rows, virt)))

    def trial_terms(relative, root):
        return pick(
            low_bit, [trial_f32[relative, pl.ds(own * root_count + root, 1), :] for own in range(occ_domain)]
        )

    own_terms = [trial_terms(0, root) for root in range(root_count)]
    live_slots = pair_count[me]
    totals = [jnp.zeros((rows, virt), F32) for _ in range(span)]
    kept = []
    for slot, (relative, first, second, energy) in enumerate(slots):
        live = live_slots > slot
        mix_first = [mixed[first, pl.ds(second * occ_domain + own, 1), :] for own in range(occ_domain)]
        mix_second = [mixed[second, pl.ds(first * occ_domain + own, 1), :] for own in range(occ_domain)]
        first_terms = pick(low_bit, mix_first)
        second_terms = pick(low_bit, mix_second)
        left = [jnp.where(own_side, own_terms[root], first_terms) for root in range(root_count)]
        right = [jnp.where(own_side, second_terms, trial_terms(relative, root)) for root in range(root_count)]
        first_by = pick(high_bit, mix_first)
        second_by = pick(high_bit, mix_second)
        weights = [(value * first_by).astype(F32) for value in left]
        parts = []
        for root in range(0, root_count, 2):
            both = jnp.dot(
                jnp.concatenate(weights[root : root + 2], axis=0).astype(BF16),
                recip[slot, :, pl.ds(root * virt, 2 * virt)],
                preferred_element_type=F32,
            )
            parts.append(both[:rows, :virt] * right[root])
            parts.append(both[rows:, virt:] * right[root + 1])
        added = group_sums(parts)
        for steps in range(1, span):
            totals[steps] += jnp.where(jnp.logical_and(live, relative == steps), added, 0.0)
        kept.append((left, [value * second_by for value in right], live))

    for steps in range(1, span):
        stage[steps - 1] = totals[steps]
    pl.semaphore_wait(barrier, 2 * (span - 1))
    copies = []
    for steps in range(1, span):
        copy = pltpu.make_async_remote_copy(
            src_ref=stage.at[steps - 1],
            dst_ref=landed.at[steps - 1],
            send_sem=send_sem.at[steps - 1],
            recv_sem=recv_sem.at[steps - 1],
            device_id={"aux": ahead(steps)},
            device_id_type=pl.DeviceIdType.MESH,
        )
        copy.start()
        copies.append(copy)

    result = totals[0]
    nothing = jnp.zeros((rows, virt), F32)
    for slot, (left, weights, live) in enumerate(kept):
        parts = []
        for root in range(0, root_count, 2):
            block = jnp.concatenate(
                [
                    jnp.concatenate([weights[root], nothing], axis=1),
                    jnp.concatenate([nothing, weights[root + 1]], axis=1),
                ],
                axis=0,
            ).astype(BF16)
            both = lax.dot_general(
                block,
                recip[slot, :, pl.ds(root * virt, 2 * virt)],
                (((1,), (1,)), ((), ())),
                preferred_element_type=F32,
            )
            parts.append(both[:rows] * left[root])
            parts.append(both[rows:] * left[root + 1])
        result += jnp.where(live, group_sums(parts), 0.0)
    for copy in copies:
        copy.wait()
    for steps in range(1, span):
        result = result + landed[steps - 1]
    for own in range(occ_domain):
        out_ref[own] = result[own * root_count : (own + 1) * root_count]


def per_device(
    ints_ov, ints_oo, trial, occ_energy, vir_energy, root_shift, vir_blocks, pair_list, pair_count
):
    slab_rows, fitting, virt = ints_ov.shape
    occ_domain = ints_oo.shape[1]
    root_count = trial.shape[1]
    slot_count = pair_list.shape[1]
    span = slab_rows // occ_domain
    rows = occ_domain * root_count
    level_table = vir_energy.reshape(-1, LANES)
    blocks = vir_blocks.T
    pairs = pair_list.transpose(1, 2, 0)
    anywhere = pl.BlockSpec(memory_space=pl.ANY)
    return pl.pallas_call(
        functools.partial(
            sigma_kernel, lax.axis_size("aux"), span, slot_count, occ_domain, root_count
        ),
        out_shape=jax.ShapeDtypeStruct((occ_domain, root_count, virt), F32),
        in_specs=[anywhere] * 9,
        out_specs=pl.BlockSpec(memory_space=pltpu.VMEM),
        scratch_shapes=[
            pltpu.VMEM(ints_ov.shape, BF16),
            pltpu.VMEM(ints_oo.shape, BF16),
            pltpu.VMEM((span * occ_domain, root_count, virt), BF16),
            pltpu.VMEM(level_table.shape, F32),
            pltpu.SMEM(occ_energy.shape, F32),
            pltpu.SMEM(root_shift.shape, F32),
            pltpu.SMEM(pair_count.shape, jnp.int32),
            pltpu.SMEM(blocks.shape, jnp.int32),
            pltpu.SMEM(pairs.shape, jnp.int32),
            pltpu.VMEM((virt, LANES), F32),
            pltpu.VMEM((span, rows, virt), F32),
            pltpu.VMEM((slab_rows, slab_rows * occ_domain, virt), F32),
            pltpu.VMEM((slot_count, virt, root_count * virt), BF16),
            pltpu.VMEM((span - 1, rows, virt), F32),
            pltpu.VMEM((span - 1, rows, virt), F32),
            pltpu.SemaphoreType.DMA,
            pltpu.SemaphoreType.DMA((8,)),
            pltpu.SemaphoreType.DMA((span - 1,)),
            pltpu.SemaphoreType.DMA((span - 1,)),
        ],
        compiler_params=pltpu.CompilerParams(collective_id=0, has_side_effects=True),
        name="sigma",
    )(ints_ov, ints_oo, trial, level_table, occ_energy, root_shift, pair_count, blocks, pairs)


def solution(mesh):
    in_specs = (
        P(("job", "aux"), None, None),
        P(("job", "aux"), None, None),
        P("job", None, None),
        P("job"),
        P("job"),
        P("job"),
        P("job", None),
        P("job", None, None),
        P("job"),
    )
    out_specs = P(("job", "aux"), None, None)
    return jax.shard_map(
        per_device, mesh=mesh, in_specs=in_specs, out_specs=out_specs, check_vma=False
    )
```

time: 16.9 us -> 14.5 us (0.86)
  Pallas kernels: 15.3 us -> 12.9 us
    pallas_call x1, Pallas kernels: 15.3 us -> 12.9 us  [per_device(): pl.pallas_call(functools.partial(sigma_kernel, lax.axis_size('aux'), span...]
where the time goes in v1:
time: 14.5 us; the launch traced here: 14.2 us
  Pallas kernels  12.9 us (89%)
  local copies, waits for them, and re-layouts  1.31 us (9%)
    pallas_call x1, Pallas kernels, per_device(): pl.pallas_call(functools.partial(sigma_kernel, lax.axis_size('aux'), span...  12.9 us
    unnamed x1, local copies, waits for them, and re-layouts  1.31 us

profile of v1, /device:TPU:0, one launch (start us, length us, event | category | flops | bytes accessed | tf_op | source)
XLA Modules:
  0.0 14.2 jit_solution(5329046495770579008)
XLA Ops:
  0.0 12.9 %sigma.1 = f32[2,4,384]{2,1,0:T(4,128)} custom-call(bf16[8,384,384]{2,1,0:T(8,128)(2,1)} %ints_hbm.1, bf16[8,2,384]{2,1,0:T(2,128)(2,1)} %couple_hbm.1, bf16[32,4,384]{2,1,0:T(4,128)(2,1)} %trial_hbm.1, f32[125,128]{1,0:T(8,128)} %bitcast.3, f32[32]{0:T(128)} %occ_hbm.1, f32[4]{0:T(128)} %shift_hbm.1, s32[16]{0:T(128)} %count_hbm.1, s32[3,16]{1,0:T(4,128)} %bitcast.5, ...), custom_call_target="tpu_custom_call" | custom-call | tf_op jit(solution)/shard_map/sigma/pallas_call | solution.py:219
  12.9 1.3 %copy.11 = f32[2,4,384]{2,1,0:T(4,128)} copy(f32[2,4,384]{2,1,0:T(4,128)} %sigma.1) | data formatting | bytes 24576

commit v2 on v1

--- a/solution.py
+++ b/solution.py
@@ -10,6 +10,10 @@
 F32 = jnp.float32
 BF16 = jnp.bfloat16
 LANES = 128
+RECIP_STEP = 6
+LOOPED = 4
+CHUNK = 8
+PAIRED = 3
 
 
 def group_sums(parts):
@@ -31,7 +35,7 @@
     ints_hbm, couple_hbm, trial_hbm, level_hbm, occ_hbm, shift_hbm, count_hbm, blocks_hbm, pairs_hbm,
     out_ref,
     ints, couple, trial, level_table, occ_energy, root_shift, pair_count, vir_blocks, pairs,
-    levels_col, trial_f32, mixed, recip, stage, landed,
+    levels_col, level_row_table, trial_f32, mixed, recip, stage, landed,
     ints_sem, small_sem, send_sem, recv_sem,
 ):
     me = lax.axis_index("aux")
@@ -61,8 +65,12 @@
             trial.at[pl.ds(steps * occ_domain, occ_domain)],
             trial_sem,
         ).start()
-    big = pltpu.make_async_copy(ints_hbm, ints, ints_sem)
-    big.start()
+    big = [
+        pltpu.make_async_copy(ints_hbm.at[pl.ds(at, CHUNK)], ints.at[pl.ds(at, CHUNK)], ints_sem.at[at // CHUNK])
+        for at in range(0, slab_rows, CHUNK)
+    ]
+    for copy in big:
+        copy.start()
 
     barrier = pltpu.get_barrier_semaphore()
     for steps in range(1, span):
@@ -71,9 +79,8 @@
                 barrier, inc=1, device_id={"aux": other}, device_id_type=pl.DeviceIdType.MESH
             )
 
-    for copy in scalars:
+    for copy in scalars[:-1]:
         copy.wait()
-    pltpu.make_async_copy(trial_hbm.at[pl.ds(0, span * occ_domain)], trial, trial_sem).wait()
 
     def level_rows(relative):
         return [level_table[pl.ds(vir_blocks[block, ahead(relative)], 1), :] for block in range(width_blocks)]
@@ -91,26 +98,53 @@
         second = relative * occ_domain + lax.rem(occ_second, occ_domain)
         slots.append((relative, first, second, occ_energy[occ_first] + occ_energy[occ_second]))
 
-    col = jnp.concatenate([levels_col[...]] * width_blocks, axis=1)
     for slot, (relative, first, second, energy) in enumerate(slots):
         level_row = jnp.concatenate(level_rows(relative), axis=1) - energy
-        for root in range(0, root_count, 2):
-            dens = [col + (level_row - root_shift[at]) for at in range(root, min(root + 2, root_count))]
-            if len(dens) == 2:
-                both = 1.0 / (dens[0] * dens[1])
-                values = [both * dens[1], both * dens[0]]
-            else:
-                values = [1.0 / dens[0]]
-            for at, value in enumerate(values):
-                recip[slot, :, pl.ds((root + at) * virt, virt)] = value.astype(BF16)
-
+        for root in range(root_count):
+            level_row_table[pl.ds(slot * root_count + root, 1), :] = level_row - root_shift[root]
+
+    def fill_recip(place, chosen):
+        start = pl.multiple_of(place * 16, 16)
+        col = levels_col[pl.ds(start, 16), :]
+        for block in range(width_blocks):
+            for slot in chosen:
+                for root in range(0, root_count, 2):
+                    dens = [
+                        col + level_row_table[pl.ds(slot * root_count + at, 1), pl.ds(block * LANES, LANES)]
+                        for at in range(root, root + 2)
+                    ]
+                    if slot % 4 >= PAIRED:
+                        values = [1.0 / den for den in dens]
+                    else:
+                        both = 1.0 / (dens[0] * dens[1])
+                        values = [both * dens[1], both * dens[0]]
+                    for at, value in enumerate(values):
+                        recip[slot, (root + at) * width_blocks + block, place] = value.astype(BF16)
+
+    def recip_rows(step, carry):
+        for piece in range(RECIP_STEP):
+            fill_recip(step * RECIP_STEP + piece, range(LOOPED))
+        return carry
+
+    lax.fori_loop(0, virt // 16 // RECIP_STEP, recip_rows, 0)
+
+    def recip_pair(slot, root):
+        return jnp.concatenate(
+            [recip[slot, root * width_blocks + at].reshape(virt, LANES) for at in range(2 * width_blocks)], axis=1
+        )
+
+    scalars[-1].wait()
+    pltpu.make_async_copy(trial_hbm.at[pl.ds(0, span * occ_domain)], trial, trial_sem).wait()
     for relative in range(span):
         for own in range(occ_domain):
             trial_f32[relative, pl.ds(own * root_count, root_count), :] = trial[relative * occ_domain + own].astype(F32)
     couple_all = jnp.concatenate([couple[row].astype(F32) for row in range(slab_rows)], axis=0).astype(BF16)
 
-    big.wait()
+    for place in range(virt // 16):
+        fill_recip(place, range(LOOPED, slot_count))
     for row in range(0, slab_rows, 2):
+        if row % CHUNK == 0:
+            big[row // CHUNK].wait()
         pair = jnp.concatenate([ints[row], ints[row + 1]], axis=1)
         both = jnp.dot(couple_all, pair, preferred_element_type=F32)
         mixed[row] = both[:, :virt]
@@ -148,7 +182,7 @@
         for root in range(0, root_count, 2):
             both = jnp.dot(
                 jnp.concatenate(weights[root : root + 2], axis=0).astype(BF16),
-                recip[slot, :, pl.ds(root * virt, 2 * virt)],
+                recip_pair(slot, root),
                 preferred_element_type=F32,
             )
             parts.append(both[:rows, :virt] * right[root])
@@ -188,7 +222,7 @@
             ).astype(BF16)
             both = lax.dot_general(
                 block,
-                recip[slot, :, pl.ds(root * virt, 2 * virt)],
+                recip_pair(slot, root),
                 (((1,), (1,)), ((), ())),
                 preferred_element_type=F32,
             )
@@ -220,7 +254,7 @@
         functools.partial(
             sigma_kernel, lax.axis_size("aux"), span, slot_count, occ_domain, root_count
         ),
-        out_shape=jax.ShapeDtypeStruct((occ_domain, root_count, virt), F32),
+        out_shape=pltpu.VMEM((occ_domain, root_count, virt), F32),
         in_specs=[anywhere] * 9,
         out_specs=pl.BlockSpec(memory_space=pltpu.VMEM),
         scratch_shapes=[
@@ -234,12 +268,13 @@
             pltpu.SMEM(blocks.shape, jnp.int32),
             pltpu.SMEM(pairs.shape, jnp.int32),
             pltpu.VMEM((virt, LANES), F32),
+            pltpu.VMEM((slot_count * root_count, virt), F32),
             pltpu.VMEM((span, rows, virt), F32),
             pltpu.VMEM((slab_rows, slab_rows * occ_domain, virt), F32),
-            pltpu.VMEM((slot_count, virt, root_count * virt), BF16),
+            pltpu.VMEM((slot_count, root_count * virt // LANES, virt // 16, 16, LANES), BF16),
             pltpu.VMEM((span - 1, rows, virt), F32),
             pltpu.VMEM((span - 1, rows, virt), F32),
-            pltpu.SemaphoreType.DMA,
+            pltpu.SemaphoreType.DMA((slab_rows // CHUNK,)),
             pltpu.SemaphoreType.DMA((8,)),
             pltpu.SemaphoreType.DMA((span - 1,)),
             pltpu.SemaphoreType.DMA((span - 1,)),

time: 14.5 us -> 11.9 us (0.82)
  Pallas kernels: 12.9 us -> 11.1 us
  local copies, waits for them, and re-layouts: 1.31 us -> 0.6 us
    pallas_call x1, Pallas kernels: 12.9 us -> 11.1 us  [per_device(): pl.pallas_call(functools.partial(sigma_kernel, lax.axis_size('aux'), span...]
    unnamed x1, local copies, waits for them, and re-layouts: 1.31 us -> 0.6 us
where the time goes in v2:
time: 11.9 us; the launch traced here: 11.7 us
  Pallas kernels  11.1 us (93%)
  local copies, waits for them, and re-layouts  0.6 us (5%)
    pallas_call x1, Pallas kernels, per_device(): pl.pallas_call(functools.partial(sigma_kernel, lax.axis_size('aux'), span...  11.1 us
    unnamed x1, local copies, waits for them, and re-layouts  0.6 us

profile of v2, /device:TPU:0, one launch (start us, length us, event | category | flops | bytes accessed | tf_op | source)
XLA Modules:
  0.0 11.7 jit_solution(6634625269388306698)
XLA Ops:
  0.0 11.1 %sigma.1 = f32[2,4,384]{2,1,0:T(4,128)S(1)} custom-call(bf16[8,384,384]{2,1,0:T(8,128)(2,1)} %ints_hbm.1, bf16[8,2,384]{2,1,0:T(2,128)(2,1)} %couple_hbm.1, bf16[32,4,384]{2,1,0:T(4,128)(2,1)} %trial_hbm.1, f32[125,128]{1,0:T(8,128)} %bitcast.3, f32[32]{0:T(128)} %occ_hbm.1, f32[4]{0:T(128)} %shift_hbm.1, s32[16]{0:T(128)} %count_hbm.1, s32[3,16]{1,0:T(4,128)} %bitcast.5, ...), custom_call_target="tpu_custom_call" | custom-call | tf_op jit(solution)/shard_map/sigma/pallas_call | solution.py:253
  11.1 0.6 %copy.11 = f32[2,4,384]{2,1,0:T(4,128)} copy(f32[2,4,384]{2,1,0:T(4,128)S(1)} %sigma.1) | data formatting | bytes 24576

commit v3 on v1

--- a/solution.py
+++ b/solution.py
@@ -10,6 +10,13 @@
 F32 = jnp.float32
 BF16 = jnp.bfloat16
 LANES = 128
+PAIRED = 2
+SPREAD = 64
+ORDER = (
+    "R00", "R01", "Wo", "D00", "D01", "R10", "R11", "D10",
+    "D11", "R20", "R21", "D20", "D21", "R30", "Wf", "Mf",
+    "R31", "D30", "D31",
+)
 
 
 def group_sums(parts):
@@ -31,7 +38,7 @@
     ints_hbm, couple_hbm, trial_hbm, level_hbm, occ_hbm, shift_hbm, count_hbm, blocks_hbm, pairs_hbm,
     out_ref,
     ints, couple, trial, level_table, occ_energy, root_shift, pair_count, vir_blocks, pairs,
-    levels_col, trial_f32, mixed, recip, stage, landed,
+    levels_col, level_row_table, spread_ref, trial_f32, mixed_own, mixed_far, couple_ref, product, recip, stage, landed,
     ints_sem, small_sem, send_sem, recv_sem,
 ):
     me = lax.axis_index("aux")
@@ -39,10 +46,18 @@
     width_blocks = virt // LANES
     rows = occ_domain * root_count
     terms = 2 * occ_domain
+    far_rows = slab_rows - occ_domain
 
     def ahead(steps):
         return lax.rem(me + steps, ndomain)
 
+    trial_sem = small_sem.at[7]
+    for steps in range(span):
+        pltpu.make_async_copy(
+            trial_hbm.at[pl.ds(ahead(steps) * occ_domain, occ_domain)],
+            trial.at[pl.ds(steps * occ_domain, occ_domain)],
+            trial_sem,
+        ).start()
     scalars = [
         pltpu.make_async_copy(src, dst, small_sem.at[at])
         for at, (src, dst) in enumerate(
@@ -54,15 +69,14 @@
     ]
     for copy in scalars:
         copy.start()
-    trial_sem = small_sem.at[len(scalars)]
-    for steps in range(span):
-        pltpu.make_async_copy(
-            trial_hbm.at[pl.ds(ahead(steps) * occ_domain, occ_domain)],
-            trial.at[pl.ds(steps * occ_domain, occ_domain)],
-            trial_sem,
-        ).start()
-    big = pltpu.make_async_copy(ints_hbm, ints, ints_sem)
-    big.start()
+    own_copy = pltpu.make_async_copy(
+        ints_hbm.at[pl.ds(0, occ_domain)], ints.at[pl.ds(0, occ_domain)], ints_sem.at[0]
+    )
+    far_copy = pltpu.make_async_copy(
+        ints_hbm.at[pl.ds(occ_domain, far_rows)], ints.at[pl.ds(occ_domain, far_rows)], ints_sem.at[1]
+    )
+    own_copy.start()
+    far_copy.start()
 
     barrier = pltpu.get_barrier_semaphore()
     for steps in range(1, span):
@@ -71,15 +85,24 @@
                 barrier, inc=1, device_id={"aux": other}, device_id_type=pl.DeviceIdType.MESH
             )
 
-    for copy in scalars:
+    def factors(shape, axis, count):
+        at = lax.broadcasted_iota(jnp.int32, shape, axis) % count
+        return jnp.exp2(at.astype(F32) * (1.0 / count))
+
+    spread = factors((SPREAD, virt), 0, SPREAD) * factors((SPREAD, virt), 1, LANES)
+    spread_ref[...] = spread
+    row_scale = factors((rows, virt), 1, SPREAD)
+    column_scale = factors((rows, virt), 1, LANES)
+
+    for copy in scalars[:-1]:
         copy.wait()
-    pltpu.make_async_copy(trial_hbm.at[pl.ds(0, span * occ_domain)], trial, trial_sem).wait()
 
     def level_rows(relative):
         return [level_table[pl.ds(vir_blocks[block, ahead(relative)], 1), :] for block in range(width_blocks)]
 
+    tall = jnp.concatenate([spread_ref[:, :LANES]] * (LANES // SPREAD), axis=0)
     for block, row in enumerate(level_rows(0)):
-        levels_col[pl.ds(block * LANES, LANES), :] = jnp.broadcast_to(row, (LANES, LANES)).T
+        levels_col[pl.ds(block * LANES, LANES), :] = jnp.broadcast_to(row, (LANES, LANES)).T * tall
 
     slots = []
     for slot in range(slot_count):
@@ -91,30 +114,43 @@
         second = relative * occ_domain + lax.rem(occ_second, occ_domain)
         slots.append((relative, first, second, occ_energy[occ_first] + occ_energy[occ_second]))
 
-    col = jnp.concatenate([levels_col[...]] * width_blocks, axis=1)
-    for slot, (relative, first, second, energy) in enumerate(slots):
+    def fill_levels(slot):
+        relative, first, second, energy = slots[slot]
         level_row = jnp.concatenate(level_rows(relative), axis=1) - energy
-        for root in range(0, root_count, 2):
-            dens = [col + (level_row - root_shift[at]) for at in range(root, min(root + 2, root_count))]
-            if len(dens) == 2:
-                both = 1.0 / (dens[0] * dens[1])
-                values = [both * dens[1], both * dens[0]]
-            else:
-                values = [1.0 / dens[0]]
-            for at, value in enumerate(values):
-                recip[slot, :, pl.ds((root + at) * virt, virt)] = value.astype(BF16)
-
-    for relative in range(span):
-        for own in range(occ_domain):
-            trial_f32[relative, pl.ds(own * root_count, root_count), :] = trial[relative * occ_domain + own].astype(F32)
-    couple_all = jnp.concatenate([couple[row].astype(F32) for row in range(slab_rows)], axis=0).astype(BF16)
-
-    big.wait()
-    for row in range(0, slab_rows, 2):
-        pair = jnp.concatenate([ints[row], ints[row + 1]], axis=1)
-        both = jnp.dot(couple_all, pair, preferred_element_type=F32)
-        mixed[row] = both[:, :virt]
-        mixed[row + 1] = both[:, virt:]
+        for root in range(root_count):
+            level_row_table[slot * root_count + root] = (level_row - root_shift[root]) * spread_ref[...]
+
+    places = virt // 16
+
+    def fill_recip(slot, root, chosen):
+        for place in chosen:
+            col = levels_col[pl.ds(place * 16, 16), :]
+            for block in range(width_blocks):
+                dens = [
+                    col
+                    + level_row_table[
+                        slot * root_count + at, pl.ds(place * 16 % SPREAD, 16), pl.ds(block * LANES, LANES)
+                    ]
+                    for at in (root, root + 1)
+                ]
+                if (place + block) % 4 < PAIRED:
+                    both = 1.0 / (dens[0] * dens[1])
+                    values = [both * dens[1], both * dens[0]]
+                else:
+                    values = [1.0 / den for den in dens]
+                for at, value in enumerate(values):
+                    recip[slot, (root + at) * width_blocks + block, place] = value.astype(BF16)
+
+    def recip_pair(slot, root):
+        return jnp.concatenate(
+            [recip[slot, root * width_blocks + at].reshape(virt, LANES) for at in range(2 * width_blocks)], axis=1
+        )
+
+    def mix(rows_pair, target):
+        pair = jnp.concatenate([ints[row] for row in rows_pair], axis=1)
+        both = jnp.dot(couple_ref[...], pair, preferred_element_type=F32)
+        target[0] = both[:, :virt]
+        target[1] = both[:, virt:]
 
     index = lax.broadcasted_iota(jnp.int32, (rows, virt), 0)
     low_bit = index % occ_domain == 0
@@ -129,37 +165,77 @@
             low_bit, [trial_f32[relative, pl.ds(own * root_count + root, 1), :] for own in range(occ_domain)]
         )
 
-    own_terms = [trial_terms(0, root) for root in range(root_count)]
+    own_terms, lefts = [], {}
+
+    def ready_own():
+        scalars[-1].wait()
+        pltpu.make_async_copy(trial_hbm.at[pl.ds(0, span * occ_domain)], trial, trial_sem).wait()
+        for relative in range(span):
+            for own in range(occ_domain):
+                trial_f32[relative, pl.ds(own * root_count, root_count), :] = trial[
+                    relative * occ_domain + own
+                ].astype(F32)
+        couple_ref[...] = jnp.concatenate([couple[row].astype(F32) for row in range(slab_rows)], axis=0).astype(BF16)
+        own_copy.wait()
+        for row in range(0, occ_domain, 2):
+            mix((row, row + 1), mixed_own.at[pl.ds(row, 2)])
+        own_terms.extend(trial_terms(0, root) for root in range(root_count))
+
+    def lefts_of(slot):
+        relative, first, second, energy = slots[slot]
+        mix_first = [mixed_own[first, pl.ds(second * occ_domain + own, 1), :] for own in range(occ_domain)]
+        first_terms = pick(low_bit, mix_first)
+        left = [jnp.where(own_side, own_terms[root], first_terms) for root in range(root_count)]
+        lefts[slot] = left, pick(high_bit, mix_first) * row_scale
+
+    def multiply(slot, root):
+        if root == 0:
+            lefts_of(slot)
+        left, first_by = lefts[slot]
+        both = jnp.dot(
+            jnp.concatenate([left[at] * first_by for at in (root, root + 1)], axis=0).astype(BF16),
+            recip_pair(slot, root),
+            preferred_element_type=F32,
+        )
+        product[slot, root] = both[:rows, :virt]
+        product[slot, root + 1] = both[rows:, virt:]
+
+    for step in ORDER:
+        kind, at = step[0], step[1:]
+        if kind == "R":
+            slot, root = int(at[0]), 2 * int(at[1])
+            if root == 0 and at[2:] != "b":
+                fill_levels(slot)
+            half = places * 2 // 3
+            fill_recip(slot, root, {"": range(places), "a": range(half), "b": range(half, places)}[at[2:]])
+        elif step == "Wo":
+            ready_own()
+        elif step == "Wf":
+            far_copy.wait()
+        elif step == "Mf":
+            for slot in range(0, slot_count, 2):
+                mix((slots[slot][2], slots[slot + 1][2]), mixed_far.at[pl.ds(slot, 2)])
+        elif kind == "D":
+            multiply(int(at[0]), 2 * int(at[1]))
+
     live_slots = pair_count[me]
     totals = [jnp.zeros((rows, virt), F32) for _ in range(span)]
     kept = []
     for slot, (relative, first, second, energy) in enumerate(slots):
         live = live_slots > slot
-        mix_first = [mixed[first, pl.ds(second * occ_domain + own, 1), :] for own in range(occ_domain)]
-        mix_second = [mixed[second, pl.ds(first * occ_domain + own, 1), :] for own in range(occ_domain)]
-        first_terms = pick(low_bit, mix_first)
+        mix_second = [
+            mixed_far[slot, pl.ds(first * occ_domain + own, 1), :] for own in range(occ_domain)
+        ]
         second_terms = pick(low_bit, mix_second)
-        left = [jnp.where(own_side, own_terms[root], first_terms) for root in range(root_count)]
+        second_by = pick(high_bit, mix_second) * column_scale
         right = [jnp.where(own_side, second_terms, trial_terms(relative, root)) for root in range(root_count)]
-        first_by = pick(high_bit, mix_first)
-        second_by = pick(high_bit, mix_second)
-        weights = [(value * first_by).astype(F32) for value in left]
-        parts = []
-        for root in range(0, root_count, 2):
-            both = jnp.dot(
-                jnp.concatenate(weights[root : root + 2], axis=0).astype(BF16),
-                recip[slot, :, pl.ds(root * virt, 2 * virt)],
-                preferred_element_type=F32,
-            )
-            parts.append(both[:rows, :virt] * right[root])
-            parts.append(both[rows:, virt:] * right[root + 1])
-        added = group_sums(parts)
+        added = group_sums([product[slot, root] * right[root] for root in range(root_count)])
         for steps in range(1, span):
             totals[steps] += jnp.where(jnp.logical_and(live, relative == steps), added, 0.0)
-        kept.append((left, [value * second_by for value in right], live))
+        kept.append((lefts[slot][0], [value * second_by for value in right], live))
 
     for steps in range(1, span):
-        stage[steps - 1] = totals[steps]
+        stage[steps - 1] = totals[steps] * column_scale
     pl.semaphore_wait(barrier, 2 * (span - 1))
     copies = []
     for steps in range(1, span):
@@ -188,13 +264,14 @@
             ).astype(BF16)
             both = lax.dot_general(
                 block,
-                recip[slot, :, pl.ds(root * virt, 2 * virt)],
+                recip_pair(slot, root),
                 (((1,), (1,)), ((), ())),
                 preferred_element_type=F32,
             )
             parts.append(both[:rows] * left[root])
             parts.append(both[rows:] * left[root + 1])
         result += jnp.where(live, group_sums(parts), 0.0)
+    result = result * row_scale
     for copy in copies:
         copy.wait()
     for steps in range(1, span):
@@ -220,7 +297,7 @@
         functools.partial(
             sigma_kernel, lax.axis_size("aux"), span, slot_count, occ_domain, root_count
         ),
-        out_shape=jax.ShapeDtypeStruct((occ_domain, root_count, virt), F32),
+        out_shape=pltpu.VMEM((occ_domain, root_count, virt), F32),
         in_specs=[anywhere] * 9,
         out_specs=pl.BlockSpec(memory_space=pltpu.VMEM),
         scratch_shapes=[
@@ -234,12 +311,17 @@
             pltpu.SMEM(blocks.shape, jnp.int32),
             pltpu.SMEM(pairs.shape, jnp.int32),
             pltpu.VMEM((virt, LANES), F32),
+            pltpu.VMEM((slot_count * root_count, SPREAD, virt), F32),
+            pltpu.VMEM((SPREAD, virt), F32),
             pltpu.VMEM((span, rows, virt), F32),
-            pltpu.VMEM((slab_rows, slab_rows * occ_domain, virt), F32),
-            pltpu.VMEM((slot_count, virt, root_count * virt), BF16),
+            pltpu.VMEM((occ_domain, slab_rows * occ_domain, virt), F32),
+            pltpu.VMEM((slot_count, slab_rows * occ_domain, virt), F32),
+            pltpu.VMEM((slab_rows * occ_domain, fitting), BF16),
+            pltpu.VMEM((slot_count, root_count, rows, virt), F32),
+            pltpu.VMEM((slot_count, root_count * virt // LANES, virt // 16, 16, LANES), BF16),
             pltpu.VMEM((span - 1, rows, virt), F32),
             pltpu.VMEM((span - 1, rows, virt), F32),
-            pltpu.SemaphoreType.DMA,
+            pltpu.SemaphoreType.DMA((2,)),
             pltpu.SemaphoreType.DMA((8,)),
             pltpu.SemaphoreType.DMA((span - 1,)),
             pltpu.SemaphoreType.DMA((span - 1,)),

time: 14.5 us -> 11.4 us (0.79); the launches traced: 14.2 us -> 11.3 us
  Pallas kernels: 12.9 us -> 10.7 us
  local copies, waits for them, and re-layouts: 1.31 us -> 0.6 us
    pallas_call x1, Pallas kernels: 12.9 us -> 10.7 us  [per_device(): pl.pallas_call(functools.partial(sigma_kernel, lax.axis_size('aux'), span...]
    unnamed x1, local copies, waits for them, and re-layouts: 1.31 us -> 0.6 us
where the time goes in v3:
time: 11.4 us; the launch traced here: 11.3 us
  Pallas kernels  10.7 us (94%)
  local copies, waits for them, and re-layouts  0.6 us (5%)
    pallas_call x1, Pallas kernels, per_device(): pl.pallas_call(functools.partial(sigma_kernel, lax.axis_size('aux'), span...  10.7 us
    unnamed x1, local copies, waits for them, and re-layouts  0.6 us

profile of v3, /device:TPU:0, one launch (start us, length us, event | category | flops | bytes accessed | tf_op | source)
XLA Modules:
  0.0 11.3 jit_solution(15148917764761745868)
XLA Ops:
  0.0 10.7 %sigma.1 = f32[2,4,384]{2,1,0:T(4,128)S(1)} custom-call(bf16[8,384,384]{2,1,0:T(8,128)(2,1)} %ints_hbm.1, bf16[8,2,384]{2,1,0:T(2,128)(2,1)} %couple_hbm.1, bf16[32,4,384]{2,1,0:T(4,128)(2,1)} %trial_hbm.1, f32[125,128]{1,0:T(8,128)} %bitcast.3, f32[32]{0:T(128)} %occ_hbm.1, f32[4]{0:T(128)} %shift_hbm.1, s32[16]{0:T(128)} %count_hbm.1, s32[3,16]{1,0:T(4,128)} %bitcast.5, ...), custom_call_target="tpu_custom_call" | custom-call | tf_op jit(solution)/shard_map/sigma/pallas_call | solution.py:296
  10.7 0.6 %copy.11 = f32[2,4,384]{2,1,0:T(4,128)} copy(f32[2,4,384]{2,1,0:T(4,128)S(1)} %sigma.1) | data formatting | bytes 24576

commit v4 on v3

--- a/solution.py
+++ b/solution.py
@@ -13,7 +13,7 @@
 PAIRED = 2
 SPREAD = 64
 ORDER = (
-    "R00", "R01", "Wo", "D00", "D01", "R10", "R11", "D10",
+    "R00", "Wo", "R01", "D00", "D01", "R10", "R11", "D10",
     "D11", "R20", "R21", "D20", "D21", "R30", "Wf", "Mf",
     "R31", "D30", "D31",
 )
@@ -123,23 +123,24 @@
     places = virt // 16
 
     def fill_recip(slot, root, chosen):
-        for place in chosen:
-            col = levels_col[pl.ds(place * 16, 16), :]
-            for block in range(width_blocks):
-                dens = [
-                    col
-                    + level_row_table[
-                        slot * root_count + at, pl.ds(place * 16 % SPREAD, 16), pl.ds(block * LANES, LANES)
-                    ]
+        for block in range(width_blocks):
+            for piece in range(0, SPREAD, 16):
+                level = [
+                    level_row_table[slot * root_count + at, pl.ds(piece, 16), pl.ds(block * LANES, LANES)]
                     for at in (root, root + 1)
                 ]
-                if (place + block) % 4 < PAIRED:
-                    both = 1.0 / (dens[0] * dens[1])
-                    values = [both * dens[1], both * dens[0]]
-                else:
-                    values = [1.0 / den for den in dens]
-                for at, value in enumerate(values):
-                    recip[slot, (root + at) * width_blocks + block, place] = value.astype(BF16)
+                for place in chosen:
+                    if place * 16 % SPREAD != piece:
+                        continue
+                    col = levels_col[pl.ds(place * 16, 16), :]
+                    dens = [col + row for row in level]
+                    if (place * 16 // SPREAD + block) % 4 < PAIRED:
+                        both = 1.0 / (dens[0] * dens[1])
+                        values = [both * dens[1], both * dens[0]]
+                    else:
+                        values = [1.0 / den for den in dens]
+                    for at, value in enumerate(values):
+                        recip[slot, (root + at) * width_blocks + block, place] = value.astype(BF16)
 
     def recip_pair(slot, root):
         return jnp.concatenate(

time: 11.4 us -> 11.4 us (level)
  no operation moved by 1% of the time
where the time goes in v4:
time: 11.4 us; the launch traced here: 11.2 us
  Pallas kernels  10.6 us (93%)
  local copies, waits for them, and re-layouts  0.6 us (5%)
    pallas_call x1, Pallas kernels, per_device(): pl.pallas_call(functools.partial(sigma_kernel, lax.axis_size('aux'), span...  10.6 us
    unnamed x1, local copies, waits for them, and re-layouts  0.6 us

profile of v4, /device:TPU:0, one launch (start us, length us, event | category | flops | bytes accessed | tf_op | source)
XLA Modules:
  0.0 11.2 jit_solution(17950015980160848161)
XLA Ops:
  0.0 10.6 %sigma.1 = f32[2,4,384]{2,1,0:T(4,128)S(1)} custom-call(bf16[8,384,384]{2,1,0:T(8,128)(2,1)} %ints_hbm.1, bf16[8,2,384]{2,1,0:T(2,128)(2,1)} %couple_hbm.1, bf16[32,4,384]{2,1,0:T(4,128)(2,1)} %trial_hbm.1, f32[125,128]{1,0:T(8,128)} %bitcast.3, f32[32]{0:T(128)} %occ_hbm.1, f32[4]{0:T(128)} %shift_hbm.1, s32[16]{0:T(128)} %count_hbm.1, s32[3,16]{1,0:T(4,128)} %bitcast.5, ...), custom_call_target="tpu_custom_call" | custom-call | tf_op jit(solution)/shard_map/sigma/pallas_call | solution.py:297
  10.6 0.6 %copy.11 = f32[2,4,384]{2,1,0:T(4,128)} copy(f32[2,4,384]{2,1,0:T(4,128)S(1)} %sigma.1) | data formatting | bytes 24576

commit v5 on v4

--- a/solution.py
+++ b/solution.py
@@ -51,13 +51,6 @@
     def ahead(steps):
         return lax.rem(me + steps, ndomain)
 
-    trial_sem = small_sem.at[7]
-    for steps in range(span):
-        pltpu.make_async_copy(
-            trial_hbm.at[pl.ds(ahead(steps) * occ_domain, occ_domain)],
-            trial.at[pl.ds(steps * occ_domain, occ_domain)],
-            trial_sem,
-        ).start()
     scalars = [
         pltpu.make_async_copy(src, dst, small_sem.at[at])
         for at, (src, dst) in enumerate(
@@ -67,7 +60,7 @@
             ]
         )
     ]
-    for copy in scalars:
+    for copy in scalars[:-1]:
         copy.start()
     own_copy = pltpu.make_async_copy(
         ints_hbm.at[pl.ds(0, occ_domain)], ints.at[pl.ds(0, occ_domain)], ints_sem.at[0]
@@ -76,6 +69,14 @@
         ints_hbm.at[pl.ds(occ_domain, far_rows)], ints.at[pl.ds(occ_domain, far_rows)], ints_sem.at[1]
     )
     own_copy.start()
+    trial_sem = small_sem.at[7]
+    for steps in range(span):
+        pltpu.make_async_copy(
+            trial_hbm.at[pl.ds(ahead(steps) * occ_domain, occ_domain)],
+            trial.at[pl.ds(steps * occ_domain, occ_domain)],
+            trial_sem,
+        ).start()
+    scalars[-1].start()
     far_copy.start()
 
     barrier = pltpu.get_barrier_semaphore()
@@ -256,10 +257,13 @@
     for slot, (left, weights, live) in enumerate(kept):
         parts = []
         for root in range(0, root_count, 2):
+            heads = [weights[at].astype(BF16).astype(F32) for at in (root, root + 1)]
+            tails = [weights[at] - head for at, head in zip((root, root + 1), heads)]
             block = jnp.concatenate(
                 [
-                    jnp.concatenate([weights[root], nothing], axis=1),
-                    jnp.concatenate([nothing, weights[root + 1]], axis=1),
+                    jnp.concatenate([half[0], nothing] if at == 0 else [nothing, half[1]], axis=1)
+                    for half in (heads, tails)
+                    for at in (0, 1)
                 ],
                 axis=0,
             ).astype(BF16)
@@ -269,6 +273,7 @@
                 (((1,), (1,)), ((), ())),
                 preferred_element_type=F32,
             )
+            both = both[: 2 * rows] + both[2 * rows :]
             parts.append(both[:rows] * left[root])
             parts.append(both[rows:] * left[root + 1])
         result += jnp.where(live, group_sums(parts), 0.0)

time: 11.4 us -> 11.4 us (level)
  no operation moved by 1% of the time
where the time goes in v5:
time: 11.4 us; the launch traced here: 11.2 us
  Pallas kernels  10.6 us (93%)
  local copies, waits for them, and re-layouts  0.6 us (5%)
    pallas_call x1, Pallas kernels, per_device(): pl.pallas_call(functools.partial(sigma_kernel, lax.axis_size('aux'), span...  10.6 us
    unnamed x1, local copies, waits for them, and re-layouts  0.6 us

profile of v5, /device:TPU:0, one launch (start us, length us, event | category | flops | bytes accessed | tf_op | source)
XLA Modules:
  0.0 11.2 jit_solution(3332172625250108296)
XLA Ops:
  0.0 10.6 %sigma.1 = f32[2,4,384]{2,1,0:T(4,128)S(1)} custom-call(bf16[8,384,384]{2,1,0:T(8,128)(2,1)} %ints_hbm.1, bf16[8,2,384]{2,1,0:T(2,128)(2,1)} %couple_hbm.1, bf16[32,4,384]{2,1,0:T(4,128)(2,1)} %trial_hbm.1, f32[125,128]{1,0:T(8,128)} %bitcast.3, f32[32]{0:T(128)} %occ_hbm.1, f32[4]{0:T(128)} %shift_hbm.1, s32[16]{0:T(128)} %count_hbm.1, s32[3,16]{1,0:T(4,128)} %bitcast.5, ...), custom_call_target="tpu_custom_call" | custom-call | tf_op jit(solution)/shard_map/sigma/pallas_call | solution.py:302
  10.6 0.6 %copy.11 = f32[2,4,384]{2,1,0:T(4,128)} copy(f32[2,4,384]{2,1,0:T(4,128)S(1)} %sigma.1) | data formatting | bytes 24576

commit v6 on v5

--- a/solution.py
+++ b/solution.py
@@ -11,7 +11,7 @@
 BF16 = jnp.bfloat16
 LANES = 128
 PAIRED = 2
-SPREAD = 64
+SPREAD = 32
 ORDER = (
     "R00", "Wo", "R01", "D00", "D01", "R10", "R11", "D10",
     "D11", "R20", "R21", "D20", "D21", "R30", "Wf", "Mf",
@@ -239,18 +239,16 @@
     for steps in range(1, span):
         stage[steps - 1] = totals[steps] * column_scale
     pl.semaphore_wait(barrier, 2 * (span - 1))
-    copies = []
     for steps in range(1, span):
         copy = pltpu.make_async_remote_copy(
             src_ref=stage.at[steps - 1],
             dst_ref=landed.at[steps - 1],
-            send_sem=send_sem.at[steps - 1],
-            recv_sem=recv_sem.at[steps - 1],
+            send_sem=send_sem,
+            recv_sem=recv_sem,
             device_id={"aux": ahead(steps)},
             device_id_type=pl.DeviceIdType.MESH,
         )
         copy.start()
-        copies.append(copy)
 
     result = totals[0]
     nothing = jnp.zeros((rows, virt), F32)
@@ -278,8 +276,8 @@
             parts.append(both[rows:] * left[root + 1])
         result += jnp.where(live, group_sums(parts), 0.0)
     result = result * row_scale
-    for copy in copies:
-        copy.wait()
+    pltpu.make_async_copy(stage, landed, send_sem).wait()
+    pltpu.make_async_copy(stage, landed, recv_sem).wait()
     for steps in range(1, span):
         result = result + landed[steps - 1]
     for own in range(occ_domain):
@@ -329,8 +327,8 @@
             pltpu.VMEM((span - 1, rows, virt), F32),
             pltpu.SemaphoreType.DMA((2,)),
             pltpu.SemaphoreType.DMA((8,)),
-            pltpu.SemaphoreType.DMA((span - 1,)),
-            pltpu.SemaphoreType.DMA((span - 1,)),
+            pltpu.SemaphoreType.DMA,
+            pltpu.SemaphoreType.DMA,
         ],
         compiler_params=pltpu.CompilerParams(collective_id=0, has_side_effects=True),
         name="sigma",

time: 11.4 us -> 11.3 us (level)
  no operation moved by 1% of the time
where the time goes in v6:
time: 11.3 us; the launch traced here: 11.1 us
  Pallas kernels  10.5 us (93%)
  local copies, waits for them, and re-layouts  0.6 us (5%)
    pallas_call x1, Pallas kernels, per_device(): pl.pallas_call(functools.partial(sigma_kernel, lax.axis_size('aux'), span...  10.5 us
    unnamed x1, local copies, waits for them, and re-layouts  0.6 us

profile of v6, /device:TPU:0, one launch (start us, length us, event | category | flops | bytes accessed | tf_op | source)
XLA Modules:
  0.0 11.1 jit_solution(3167063982024828169)
XLA Ops:
  0.0 10.5 %sigma.1 = f32[2,4,384]{2,1,0:T(4,128)S(1)} custom-call(bf16[8,384,384]{2,1,0:T(8,128)(2,1)} %ints_hbm.1, bf16[8,2,384]{2,1,0:T(2,128)(2,1)} %couple_hbm.1, bf16[32,4,384]{2,1,0:T(4,128)(2,1)} %trial_hbm.1, f32[125,128]{1,0:T(8,128)} %bitcast.3, f32[32]{0:T(128)} %occ_hbm.1, f32[4]{0:T(128)} %shift_hbm.1, s32[16]{0:T(128)} %count_hbm.1, s32[3,16]{1,0:T(4,128)} %bitcast.5, ...), custom_call_target="tpu_custom_call" | custom-call | tf_op jit(solution)/shard_map/sigma/pallas_call | solution.py:300
  10.5 0.6 %copy.11 = f32[2,4,384]{2,1,0:T(4,128)} copy(f32[2,4,384]{2,1,0:T(4,128)S(1)} %sigma.1) | data formatting | bytes 24576

commit v7 on v6

--- a/solution.py
+++ b/solution.py
@@ -236,10 +236,9 @@
             totals[steps] += jnp.where(jnp.logical_and(live, relative == steps), added, 0.0)
         kept.append((lefts[slot][0], [value * second_by for value in right], live))
 
-    for steps in range(1, span):
+    pl.semaphore_wait(barrier, 2 * (span - 1))
+    for steps in sorted(range(1, span), key=lambda steps: (steps == 1, steps)):
         stage[steps - 1] = totals[steps] * column_scale
-    pl.semaphore_wait(barrier, 2 * (span - 1))
-    for steps in range(1, span):
         copy = pltpu.make_async_remote_copy(
             src_ref=stage.at[steps - 1],
             dst_ref=landed.at[steps - 1],

time: 11.3 us -> 11.3 us (level)
  no operation moved by 1% of the time
where the time goes in v7:
time: 11.3 us; the launch traced here: 11.1 us
  Pallas kernels  10.5 us (93%)
  local copies, waits for them, and re-layouts  0.6 us (5%)
    pallas_call x1, Pallas kernels, per_device(): pl.pallas_call(functools.partial(sigma_kernel, lax.axis_size('aux'), span...  10.5 us
    unnamed x1, local copies, waits for them, and re-layouts  0.6 us

profile of v7, /device:TPU:0, one launch (start us, length us, event | category | flops | bytes accessed | tf_op | source)
XLA Modules:
  0.0 11.1 jit_solution(13581247045590887508)
XLA Ops:
  0.0 10.5 %sigma.1 = f32[2,4,384]{2,1,0:T(4,128)S(1)} custom-call(bf16[8,384,384]{2,1,0:T(8,128)(2,1)} %ints_hbm.1, bf16[8,2,384]{2,1,0:T(2,128)(2,1)} %couple_hbm.1, bf16[32,4,384]{2,1,0:T(4,128)(2,1)} %trial_hbm.1, f32[125,128]{1,0:T(8,128)} %bitcast.3, f32[32]{0:T(128)} %occ_hbm.1, f32[4]{0:T(128)} %shift_hbm.1, s32[16]{0:T(128)} %count_hbm.1, s32[3,16]{1,0:T(4,128)} %bitcast.5, ...), custom_call_target="tpu_custom_call" | custom-call | tf_op jit(solution)/shard_map/sigma/pallas_call | solution.py:299
  10.5 0.6 %copy.11 = f32[2,4,384]{2,1,0:T(4,128)} copy(f32[2,4,384]{2,1,0:T(4,128)S(1)} %sigma.1) | data formatting | bytes 24576

commit v8 on v7

--- a/solution.py
+++ b/solution.py
@@ -68,7 +68,7 @@
     far_copy = pltpu.make_async_copy(
         ints_hbm.at[pl.ds(occ_domain, far_rows)], ints.at[pl.ds(occ_domain, far_rows)], ints_sem.at[1]
     )
-    own_copy.start()
+    own_copy.start(priority=1)
     trial_sem = small_sem.at[7]
     for steps in range(span):
         pltpu.make_async_copy(
@@ -77,7 +77,7 @@
             trial_sem,
         ).start()
     scalars[-1].start()
-    far_copy.start()
+    far_copy.start(priority=1)
 
     barrier = pltpu.get_barrier_semaphore()
     for steps in range(1, span):

time: 11.3 us -> 11.3 us (level)
  no operation moved by 1% of the time
where the time goes in v8:
time: 11.3 us; the launch traced here: 11.1 us
  Pallas kernels  10.5 us (93%)
  local copies, waits for them, and re-layouts  0.6 us (5%)
    pallas_call x1, Pallas kernels, per_device(): pl.pallas_call(functools.partial(sigma_kernel, lax.axis_size('aux'), span...  10.5 us
    unnamed x1, local copies, waits for them, and re-layouts  0.6 us

profile of v8, /device:TPU:0, one launch (start us, length us, event | category | flops | bytes accessed | tf_op | source)
XLA Modules:
  0.0 11.1 jit_solution(17255959250861540578)
XLA Ops:
  0.0 10.5 %sigma.1 = f32[2,4,384]{2,1,0:T(4,128)S(1)} custom-call(bf16[8,384,384]{2,1,0:T(8,128)(2,1)} %ints_hbm.1, bf16[8,2,384]{2,1,0:T(2,128)(2,1)} %couple_hbm.1, bf16[32,4,384]{2,1,0:T(4,128)(2,1)} %trial_hbm.1, f32[125,128]{1,0:T(8,128)} %bitcast.3, f32[32]{0:T(128)} %occ_hbm.1, f32[4]{0:T(128)} %shift_hbm.1, s32[16]{0:T(128)} %count_hbm.1, s32[3,16]{1,0:T(4,128)} %bitcast.5, ...), custom_call_target="tpu_custom_call" | custom-call | tf_op jit(solution)/shard_map/sigma/pallas_call | solution.py:299
  10.5 0.6 %copy.11 = f32[2,4,384]{2,1,0:T(4,128)} copy(f32[2,4,384]{2,1,0:T(4,128)S(1)} %sigma.1) | data formatting | bytes 24576
